TPU v7x, 128 devices: a whole 4x4x4 slice. The times are simulated.
128 devices in a mesh: row: 8 (over x, core), col: 16 (over y, z).
Axes of the slice: x: 4, y: 4, z: 4, core: 2. Of those that a mesh axis runs over, the one named last changes fastest.
Arguments:
- w_rec: bfloat16 [2, 4096, 4, 4096], P(None, 'row', None, 'col'), may hold values from -0.09375 to 0.09375
- w_in: bfloat16 [2, 4096, 4, 4096], P(None, 'row', None, 'col'), may hold values from -0.09375 to 0.09375
- gate_pre: float32 [2, 6, 64, 4, 4096], P(None, None, None, None, 'col'), may hold values from -8 to 8, as said below
- cells: float32 [2, 7, 64, 4096], P(None, None, None, 'col'), may hold values from -6 to 6
- layer_in: bfloat16 [2, 6, 64, 4096], P(None, None, None, 'row'), may hold values from -1 to 1
- h_prev: bfloat16 [2, 6, 64, 4096], P(None, None, None, 'row'), may hold values from -1 to 1
- top_grad: float32 [6, 64, 4096], P(None, None, 'col'), may hold values from -40 to 40
Outputs:
- w_rec_grad: bfloat16 [2, 4096, 4, 4096], P(None, 'row', None, 'col')
- w_in_grad: bfloat16 [2, 4096, 4, 4096], P(None, 'row', None, 'col')
- input_grad: float32 [6, 64, 4096], P(None, None, 'col')
Inputs may be any that keep to these rules, and one draw needn't show every extreme that they name: `gate_pre`: dimension 3 holds the input, forget, candidate and output gates in that order.
All inputs are finite; a program needn't handle non-finite values.
Results may differ from a plain program's by a relative error of at most 0.0051.
Values sent between devices are 32-bit elements; how exact they have to be, the bound alone decides.
A program may use at most 128 MiB of HBM per device.

v0:
```python
import jax
import jax.numpy as jnp
from jax import lax
from jax.sharding import Mesh
from jax.sharding import PartitionSpec as P

WIDTH = 4096
LAYERS = 2
COL = ("col_0", "col_1")
ROW = ("row_0", "row_1")
ROW_COL = ("row_0", "row_1", "col_0", "col_1")


def total_of_pieces(x, axis):
    return lax.all_gather(x, axis).sum(0)


def from_root(x, axis, root):
    return lax.dynamic_index_in_dim(lax.all_gather(x, axis), root, 0, keepdims=False)


def by_axis(x, axes):
    for axis in axes:
        x = lax.psum(x, axis)
    return x


def cell_backward(preact, cell_prev, cell_now, hid_grad, cell_carry):
    in_gate = jax.nn.sigmoid(preact[:, 0])
    forget = jax.nn.sigmoid(preact[:, 1])
    cand_gate = jnp.tanh(preact[:, 2])
    out_gate = jax.nn.sigmoid(preact[:, 3])
    tanh_cell = jnp.tanh(cell_now)
    cell_grad = cell_carry + hid_grad * out_gate * (1.0 - tanh_cell * tanh_cell)
    grad_in = cell_grad * cand_gate * in_gate * (1.0 - in_gate)
    grad_forget = cell_grad * cell_prev * forget * (1.0 - forget)
    grad_cand = cell_grad * in_gate * (1.0 - cand_gate * cand_gate)
    grad_out = hid_grad * tanh_cell * out_gate * (1.0 - out_gate)
    gate_grads = jnp.stack([grad_in, grad_forget, grad_cand, grad_out], axis=1).astype(jnp.bfloat16)
    return (gate_grads, cell_grad * forget)


def contract_gates(gate_flat, weight_flat):
    return lax.dot_general(
        gate_flat, weight_flat, (((1,), (1,)), ((), ())), preferred_element_type=jnp.float32
    )


def own_block(total):
    ratio = lax.axis_size(COL) // lax.axis_size(ROW)
    width = total.shape[-1] // ratio
    column = lax.axis_index(COL)
    piece = lax.dynamic_slice_in_dim(total, column % ratio * width, width, total.ndim - 1)
    return (piece, column // ratio)


def wave_units(partial_value):
    piece, root = own_block(total_of_pieces(partial_value, COL))
    return from_root(piece, ROW, root)


def input_units(partial_value):
    piece, root = own_block(lax.psum(partial_value, COL))
    return from_root(piece, ROW, root)


def local(w_rec, w_in, gate_pre, cells, layer_in, h_prev, top_grad):
    layers = w_rec.shape[0]
    row_units = w_rec.shape[1]
    steps, batch, col_units = top_grad.shape
    rec_flats = [w_rec[layer].reshape(row_units, 4 * col_units) for layer in range(layers)]
    in_flats = [w_in[layer].reshape(row_units, 4 * col_units) for layer in range(layers)]
    gate_store = [None] * layers
    zeros = jnp.zeros((layers, batch, col_units), jnp.float32)
    empty = tuple(
        (jnp.zeros((steps, batch, 4, col_units), jnp.bfloat16) for layer in range(layers))
    )

    def diagonal_step(diagonal, carry):
        rec_carry, cell_carry, above, stores = carry
        partials = []
        dx_partials = []
        new_cells = []
        new_stores = []
        for layer in range(layers):
            depth = layers - 1 - layer
            step_idx = steps - 1 - diagonal + depth
            valid = (step_idx >= 0) & (step_idx < steps)
            clamped = jnp.clip(step_idx, 0, steps - 1).astype(jnp.int32)
            preact = lax.dynamic_index_in_dim(gate_pre[layer], clamped, 0, keepdims=False)
            cell_prev = lax.dynamic_index_in_dim(cells[layer], clamped, 0, keepdims=False)
            cell_now = lax.dynamic_index_in_dim(cells[layer], clamped + 1, 0, keepdims=False)
            if layer == layers - 1:
                outside = lax.dynamic_index_in_dim(top_grad, clamped, 0, keepdims=False)
            else:
                outside = above[layer]
            gate_grads, cell_next = cell_backward(
                preact, cell_prev, cell_now, outside + rec_carry[layer], cell_carry[layer]
            )
            gate_grads = jnp.where(valid, gate_grads, jnp.zeros_like(gate_grads))
            cell_next = jnp.where(valid, cell_next, jnp.zeros_like(cell_next))
            previous = lax.dynamic_index_in_dim(stores[layer], clamped, 0, keepdims=False)
            written = jnp.where(valid, gate_grads, previous)
            new_stores.append(lax.dynamic_update_index_in_dim(stores[layer], written, clamped, 0))
            gate_flat = gate_grads.reshape(batch, 4 * col_units)
            partials.append(contract_gates(gate_flat, rec_flats[layer]))
            if layer > 0:
                dx_partials.append(contract_gates(gate_flat, in_flats[layer]))
            new_cells.append(cell_next)
        units = wave_units(jnp.concatenate(partials + dx_partials, axis=0))
        rec_next = jnp.stack(
            [units[layer * batch : (layer + 1) * batch] for layer in range(layers)]
        )
        above_list = [units[layers * batch : (layers + 1) * batch]]
        above_next = jnp.stack(above_list + [jnp.zeros((batch, col_units), jnp.float32)])
        return (rec_next, jnp.stack(new_cells), above_next, tuple(new_stores))

    final = lax.fori_loop(0, steps + layers - 1, diagonal_step, (zeros, zeros, zeros, empty))
    for layer in range(layers):
        gate_store[layer] = final[3][layer].reshape(steps * batch, 4 * col_units)
    input_grad = input_units(contract_gates(gate_store[0], in_flats[0])).reshape(
        steps, batch, col_units
    )
    rec_grads = []
    in_grads = []
    partial_sums = []
    for layer in range(layers):
        raw_rec = lax.dot_general(
            h_prev[layer].reshape(steps * batch, row_units),
            gate_store[layer],
            (((0,), (0,)), ((), ())),
            preferred_element_type=jnp.float32,
        )
        raw_in = lax.dot_general(
            layer_in[layer].reshape(steps * batch, row_units),
            gate_store[layer],
            (((0,), (0,)), ((), ())),
            preferred_element_type=jnp.float32,
        )
        rec_grads.append(raw_rec)
        in_grads.append(raw_in)
        partial_sums.append(jnp.sum(raw_rec * raw_rec) + jnp.sum(raw_in * raw_in))
    totals = [by_axis(partial_value, ROW_COL) for partial_value in partial_sums]
    sumsq = totals[0]
    for extra in totals[1:]:
        sumsq = sumsq + extra
    scale = 1.0 / jnp.maximum(jnp.sqrt(sumsq / (8.0 * LAYERS * WIDTH * WIDTH)), 0.05)
    w_rec_grad = jnp.stack(
        [(rec_grads[layer] * scale).reshape(row_units, 4, col_units) for layer in range(layers)]
    ).astype(jnp.bfloat16)
    w_in_grad = jnp.stack(
        [(in_grads[layer] * scale).reshape(row_units, 4, col_units) for layer in range(layers)]
    ).astype(jnp.bfloat16)
    return (w_rec_grad, w_in_grad, input_grad)


def solution(mesh):
    torus = Mesh(mesh.devices.reshape(4, 2, 4, 4), ("row_0", "row_1", "col_0", "col_1"))
    placed = (
        P(None, ROW, None, COL),
        P(None, ROW, None, COL),
        P(None, None, None, None, COL),
        P(None, None, None, COL),
        P(None, None, None, ROW),
        P(None, None, None, ROW),
        P(None, None, COL),
    )
    return jax.shard_map(
        local,
        mesh=torus,
        in_specs=placed,
        out_specs=(P(None, ROW, None, COL), P(None, ROW, None, COL), P(None, None, COL)),
        check_vma=False,
    )
```

profile of v0, /device:TPU:1, one launch (start us, length us, event | category | flops | bytes accessed | tf_op | source)
XLA Modules:
  0.0 909.9 jit_solution(18277390417767794821)
XLA Ops:
  8.0 2.3 fusion.49
  10.3 1.2 copy.32
  11.5 1.2 copy.33
  12.7 1.7 fusion.48
  14.4 1.3 copy.34
  16.2 1.2 broadcast.490.clone
  17.4 1.1 broadcast.490.clone2
  19.8 720.3 %while.24 = (s32[]{:T(128)}, f32[2,64,256]{2,1,0:T(8,128)}, f32[2,64,256]{2,1,0:T(8,128)S(1)}, f32[2,64,256]{2,1,0:T(8,128)}, bf16[6,64,4,256]{3,2,1,0:T(4,128)(...) while((s32[]{:T(128)}, f32[2,64,256]{2,1,0:T(8,128)}, ...), condition=%wide.region_2.3_spmd, body=%wide.region_0.2_spmd.sunk | while | flops 205930528 | bytes 71566664 | solution.py:118
  22.0 1.9 fusion.97
  24.0 1.3 multiply_convert_fusion.9
  30.1 64.5 %all-gather.13.cloned.1.call-done = f32[3072,512]{1,0:T(8,128)} async-done(((f32[192,512]{1,0:T(8,128)}), f32[3072,512]{1,0:T(8,128)}) %all-gather.13.cloned.1.call-update) | async-done | bytes 6291472 | tf_op jit(solution)/shard_map/while/body/eval_jaxpr/all_gather | solution.py:15
  94.6 3.5 reduce_sum.62
  104.3 19.1 %all-gather.15.cloned.1.call-done = f32[1536,256]{1,0:T(8,128)} async-done(((f32[192,256]{1,0:T(8,128)}), f32[1536,256]{1,0:T(8,128)}) %all-gather.15.cloned.1.call-update) | async-done | bytes 1572880 | tf_op jit(solution)/shard_map/while/body/eval_jaxpr/all_gather | solution.py:19
  127.8 1.9 fusion.97
  129.7 1.3 multiply_convert_fusion.9
  135.9 61.1 %all-gather.13.cloned.1.call-done = f32[3072,512]{1,0:T(8,128)} async-done(((f32[192,512]{1,0:T(8,128)}), f32[3072,512]{1,0:T(8,128)}) %all-gather.13.cloned.1.call-update) | async-done | bytes 6291472 | tf_op jit(solution)/shard_map/while/body/eval_jaxpr/all_gather | solution.py:15
  197.0 3.5 reduce_sum.62
  206.7 19.1 %all-gather.15.cloned.1.call-done = f32[1536,256]{1,0:T(8,128)} async-done(((f32[192,256]{1,0:T(8,128)}), f32[1536,256]{1,0:T(8,128)}) %all-gather.15.cloned.1.call-update) | async-done | bytes 1572880 | tf_op jit(solution)/shard_map/while/body/eval_jaxpr/all_gather | solution.py:19
  230.2 1.9 fusion.97
  232.2 1.3 multiply_convert_fusion.9
  238.3 61.1 %all-gather.13.cloned.1.call-done = f32[3072,512]{1,0:T(8,128)} async-done(((f32[192,512]{1,0:T(8,128)}), f32[3072,512]{1,0:T(8,128)}) %all-gather.13.cloned.1.call-update) | async-done | bytes 6291472 | tf_op jit(solution)/shard_map/while/body/eval_jaxpr/all_gather | solution.py:15
  299.4 3.5 reduce_sum.62
  309.1 19.1 %all-gather.15.cloned.1.call-done = f32[1536,256]{1,0:T(8,128)} async-done(((f32[192,256]{1,0:T(8,128)}), f32[1536,256]{1,0:T(8,128)}) %all-gather.15.cloned.1.call-update) | async-done | bytes 1572880 | tf_op jit(solution)/shard_map/while/body/eval_jaxpr/all_gather | solution.py:19
  332.7 1.9 fusion.97
  334.6 1.3 multiply_convert_fusion.9
  340.7 61.1 %all-gather.13.cloned.1.call-done = f32[3072,512]{1,0:T(8,128)} async-done(((f32[192,512]{1,0:T(8,128)}), f32[3072,512]{1,0:T(8,128)}) %all-gather.13.cloned.1.call-update) | async-done | bytes 6291472 | tf_op jit(solution)/shard_map/while/body/eval_jaxpr/all_gather | solution.py:15
  401.8 3.5 reduce_sum.62
  411.5 19.1 %all-gather.15.cloned.1.call-done = f32[1536,256]{1,0:T(8,128)} async-done(((f32[192,256]{1,0:T(8,128)}), f32[1536,256]{1,0:T(8,128)}) %all-gather.15.cloned.1.call-update) | async-done | bytes 1572880 | tf_op jit(solution)/shard_map/while/body/eval_jaxpr/all_gather | solution.py:19
  435.1 1.9 fusion.97
  437.0 1.3 multiply_convert_fusion.9
  443.1 61.1 %all-gather.13.cloned.1.call-done = f32[3072,512]{1,0:T(8,128)} async-done(((f32[192,512]{1,0:T(8,128)}), f32[3072,512]{1,0:T(8,128)}) %all-gather.13.cloned.1.call-update) | async-done | bytes 6291472 | tf_op jit(solution)/shard_map/while/body/eval_jaxpr/all_gather | solution.py:15
  504.2 3.5 reduce_sum.62
  513.9 19.1 %all-gather.15.cloned.1.call-done = f32[1536,256]{1,0:T(8,128)} async-done(((f32[192,256]{1,0:T(8,128)}), f32[1536,256]{1,0:T(8,128)}) %all-gather.15.cloned.1.call-update) | async-done | bytes 1572880 | tf_op jit(solution)/shard_map/while/body/eval_jaxpr/all_gather | solution.py:19
  537.5 1.9 fusion.97
  539.4 1.3 multiply_convert_fusion.9
  545.5 61.1 %all-gather.13.cloned.1.call-done = f32[3072,512]{1,0:T(8,128)} async-done(((f32[192,512]{1,0:T(8,128)}), f32[3072,512]{1,0:T(8,128)}) %all-gather.13.cloned.1.call-update) | async-done | bytes 6291472 | tf_op jit(solution)/shard_map/while/body/eval_jaxpr/all_gather | solution.py:15
  606.7 3.5 reduce_sum.62
  616.3 19.1 %all-gather.15.cloned.1.call-done = f32[1536,256]{1,0:T(8,128)} async-done(((f32[192,256]{1,0:T(8,128)}), f32[1536,256]{1,0:T(8,128)}) %all-gather.15.cloned.1.call-update) | async-done | bytes 1572880 | tf_op jit(solution)/shard_map/while/body/eval_jaxpr/all_gather | solution.py:19
  639.9 1.9 fusion.97
  641.8 1.3 multiply_convert_fusion.9
  647.9 61.1 %all-gather.13.cloned.1.call-done = f32[3072,512]{1,0:T(8,128)} async-done(((f32[192,512]{1,0:T(8,128)}), f32[3072,512]{1,0:T(8,128)}) %all-gather.13.cloned.1.call-update) | async-done | bytes 6291472 | tf_op jit(solution)/shard_map/while/body/eval_jaxpr/all_gather | solution.py:15
  709.1 3.5 reduce_sum.62
  718.8 19.1 %all-gather.15.cloned.1.call-done = f32[1536,256]{1,0:T(8,128)} async-done(((f32[192,256]{1,0:T(8,128)}), f32[1536,256]{1,0:T(8,128)}) %all-gather.15.cloned.1.call-update) | async-done | bytes 1572880 | tf_op jit(solution)/shard_map/while/body/eval_jaxpr/all_gather | solution.py:19
  740.1 1.4 copy.35
  741.8 1.5 fusion.55
  743.4 85.0 %all-reduce.3.cloned.1.call-done = f32[384,512]{1,0:T(8,128)} async-done(((f32[384,512]{1,0:T(8,128)}), f32[384,512]{1,0:T(8,128)}) %all-reduce.3.cloned.1.call-update) | async-done | bytes 786448 | tf_op jit(solution)/shard_map/psum | solution.py:63
  828.4 1.8 constant_dynamic-slice_fusion.7
  832.1 1.6 multiply_reduce_fusion.3
  833.7 2.7 multiply_reduce_fusion.2
  837.7 3.9 multiply_reduce_fusion.1
  841.6 2.7 multiply_reduce_fusion
  845.6 9.7 %psum.75 = f32[]{:T(128)} all-reduce(f32[]{:T(128)S(6)} %add.517), channel_id=1, replica_groups=mesh['row_0'=4,'row_1'=2,'col_0'=4,'col_1'=4] {'row_0'}, use_global_device_ids=true, to_apply=%region_5.6 | all-reduce | flops 1 | bytes 8 | tf_op jit(solution)/shard_map/psum | solution.py:24
  855.3 6.7 psum.74
  862.1 8.7 psum.73
  870.7 7.5 psum.72
  879.0 4.1 multiply_convert_fusion.4
  883.1 2.4 copy.22
  885.5 2.4 copy.23
  887.9 3.5 multiply_convert_fusion.6
  891.3 2.5 copy.20
  893.9 1.4 copy.21
  895.3 2.8 pad_maximum_fusion.4
  898.2 2.8 pad_maximum_fusion.3
  901.0 1.8 constant_dynamic-slice_fusion.6
  (408 shorter events, 110.6 us)
Async XLA Ops:
  10.3 2.4 copy-start.22
  12.7 3.0 copy-start.21
  19.8 74.8 %all-gather.13.cloned.1.call-start = ((), (), s32[]{:S(2)}) async-start(), calls=%async_computation.2 | async-start | bytes 6684672 | tf_op jit(solution)/shard_map/while/body/eval_jaxpr/all_gather | solution.py:15
  22.0 3.2 copy-start
  22.0 5.8 copy-start.3
  24.0 4.3 copy-start.2
  25.2 2.1 copy-start.5
  25.2 2.1 copy-start.6
  25.2 2.1 copy-start.7
  25.3 2.1 copy-start.8
  26.2 2.5 copy-start.1
  30.0 93.4 %all-gather.15.cloned.1.call-start = ((), (), s32[]{:S(2)}) async-start(), calls=%async_computation.3 | async-start | bytes 1769472 | tf_op jit(solution)/shard_map/while/body/eval_jaxpr/all_gather | solution.py:19
  125.6 71.4 %all-gather.13.cloned.1.call-start = ((), (), s32[]{:S(2)}) async-start(), calls=%async_computation.2 | async-start | bytes 6684672 | tf_op jit(solution)/shard_map/while/body/eval_jaxpr/all_gather | solution.py:15
  127.8 3.2 copy-start
  127.8 5.8 copy-start.3
  129.7 4.3 copy-start.2
  131.0 2.1 copy-start.5
  131.0 2.1 copy-start.6
  131.0 2.1 copy-start.7
  131.0 2.1 copy-start.8
  132.0 2.5 copy-start.1
  135.8 90.0 %all-gather.15.cloned.1.call-start = ((), (), s32[]{:S(2)}) async-start(), calls=%async_computation.3 | async-start | bytes 1769472 | tf_op jit(solution)/shard_map/while/body/eval_jaxpr/all_gather | solution.py:19
  228.0 71.4 %all-gather.13.cloned.1.call-start = ((), (), s32[]{:S(2)}) async-start(), calls=%async_computation.2 | async-start | bytes 6684672 | tf_op jit(solution)/shard_map/while/body/eval_jaxpr/all_gather | solution.py:15
  230.2 3.2 copy-start
  230.2 5.8 copy-start.3
  232.2 4.3 copy-start.2
  233.4 2.1 copy-start.5
  234.4 2.5 copy-start.1
  238.2 90.0 %all-gather.15.cloned.1.call-start = ((), (), s32[]{:S(2)}) async-start(), calls=%async_computation.3 | async-start | bytes 1769472 | tf_op jit(solution)/shard_map/while/body/eval_jaxpr/all_gather | solution.py:19
  330.4 71.4 %all-gather.13.cloned.1.call-start = ((), (), s32[]{:S(2)}) async-start(), calls=%async_computation.2 | async-start | bytes 6684672 | tf_op jit(solution)/shard_map/while/body/eval_jaxpr/all_gather | solution.py:15
  332.7 3.2 copy-start
  332.7 5.8 copy-start.3
  334.6 4.3 copy-start.2
  336.8 2.5 copy-start.1
  340.6 90.0 %all-gather.15.cloned.1.call-start = ((), (), s32[]{:S(2)}) async-start(), calls=%async_computation.3 | async-start | bytes 1769472 | tf_op jit(solution)/shard_map/while/body/eval_jaxpr/all_gather | solution.py:19
  432.8 71.4 %all-gather.13.cloned.1.call-start = ((), (), s32[]{:S(2)}) async-start(), calls=%async_computation.2 | async-start | bytes 6684672 | tf_op jit(solution)/shard_map/while/body/eval_jaxpr/all_gather | solution.py:15
  435.1 3.2 copy-start
  435.1 5.8 copy-start.3
  437.0 4.3 copy-start.2
  439.2 2.5 copy-start.1
  443.0 90.0 %all-gather.15.cloned.1.call-start = ((), (), s32[]{:S(2)}) async-start(), calls=%async_computation.3 | async-start | bytes 1769472 | tf_op jit(solution)/shard_map/while/body/eval_jaxpr/all_gather | solution.py:19
  535.3 71.4 %all-gather.13.cloned.1.call-start = ((), (), s32[]{:S(2)}) async-start(), calls=%async_computation.2 | async-start | bytes 6684672 | tf_op jit(solution)/shard_map/while/body/eval_jaxpr/all_gather | solution.py:15
  537.5 3.2 copy-start
  537.5 5.8 copy-start.3
  539.4 4.3 copy-start.2
  541.6 2.5 copy-start.1
  545.4 90.0 %all-gather.15.cloned.1.call-start = ((), (), s32[]{:S(2)}) async-start(), calls=%async_computation.3 | async-start | bytes 1769472 | tf_op jit(solution)/shard_map/while/body/eval_jaxpr/all_gather | solution.py:19
  637.7 71.4 %all-gather.13.cloned.1.call-start = ((), (), s32[]{:S(2)}) async-start(), calls=%async_computation.2 | async-start | bytes 6684672 | tf_op jit(solution)/shard_map/while/body/eval_jaxpr/all_gather | solution.py:15
  639.9 3.2 copy-start
  639.9 5.8 copy-start.3
  641.8 4.3 copy-start.2
  644.1 2.5 copy-start.1
  647.9 90.0 %all-gather.15.cloned.1.call-start = ((), (), s32[]{:S(2)}) async-start(), calls=%async_computation.3 | async-start | bytes 1769472 | tf_op jit(solution)/shard_map/while/body/eval_jaxpr/all_gather | solution.py:19
  740.1 88.3 %all-reduce.3.cloned.1.call-start = ((), (), s32[]{:S(2)}) async-start(), calls=%async_computation | async-start | bytes 1572864 | tf_op jit(solution)/shard_map/psum | solution.py:63
  741.8 88.4 %copy-start.14 = (bf16[6,64,4,256]{3,2,1,0:T(4,128)(2,1)S(1)}, bf16[6,64,4,256]{3,2,1,0:T(4,128)(2,1)}, u32[]{:S(2)}) copy-start(bf16[6,64,4,256]{3,2,1,0:T(4,128)(2,1)} %get-tuple-element.336) | copy-start | bytes 2359300
  743.3 88.0 %copy-start.23 = (bf16[2,6,64,512]{3,2,1,0:T(8,128)(2,1)S(1)}, bf16[2,6,64,512]{3,2,1,0:T(8,128)(2,1)}, u32[]{:S(2)}) copy-start(bf16[2,6,64,512]{3,2,1,0:T(8,128)(2,1)} %param.14) | copy-start | bytes 2359300
  743.3 157.7 %all-gather.11.cloned.1.call-start = ((), (), s32[]{:S(2)}) async-start(), calls=%async_computation.1 | async-start | bytes 3538944 | tf_op jit(solution)/shard_map/all_gather | solution.py:19
  743.4 88.7 %copy-start.24 = (bf16[2,6,64,512]{3,2,1,0:T(8,128)(2,1)S(1)}, bf16[2,6,64,512]{3,2,1,0:T(8,128)(2,1)}, u32[]{:S(2)}) copy-start(bf16[2,6,64,512]{3,2,1,0:T(8,128)(2,1)} %param.13) | copy-start | bytes 2359300
  836.4 5.2 copy-start.13
  891.3 2.5 copy-start.15
  891.3 4.0 copy-start.17
  891.3 4.0 copy-start.18
  895.3 2.9 copy-start.19
  895.3 2.9 copy-start.20
  (55 other events, 73.6 us)
Sparse Core Ops, SparseCore 0:
  30.1 64.4 all-gather.12
  98.9 24.3 all-gather.14
  135.9 61.0 all-gather.12
  201.4 24.3 all-gather.14
  238.3 61.0 all-gather.12
  303.8 24.3 all-gather.14
  340.7 61.0 all-gather.12
  406.2 24.3 all-gather.14
  443.1 61.0 all-gather.12
  508.6 24.3 all-gather.14
  545.6 61.0 all-gather.12
  611.0 24.3 all-gather.14
  648.0 61.0 all-gather.12
  713.4 24.3 all-gather.14
Sparse Core Ops, SparseCore 1:
  744.4 83.9 all-reduce.2
  830.3 29.2 all-gather.10
where the time goes:
time: 917 us; the launch traced here: 910 us
  waiting for transfers between devices  650 us (71%)
  other arithmetic  102 us (11%)
  local copies, waits for them, and re-layouts  82.5 us (9%)
  blocking collectives  32.6 us (4%)
  matrix products  21.7 us (2%)
  between operations  18.6 us (2%)
    all_gather x7, waiting for transfers between devices, total_of_pieces(): return lax.all_gather(x, axis).sum(0)  431 us
    all_gather x8, waiting for transfers between devices, from_root(): lax.all_gather(x, axis)  134 us
    psum x1, waiting for transfers between devices, input_units(): piece, root = own_block(lax.psum(partial_value, COL))  85 us
    psum x4, blocking collectives, by_axis(): x = lax.psum(x, axis)  32.6 us
    another operation x23, other arithmetic  29.7 us
    reduce_sum x7, other arithmetic, total_of_pieces(): return lax.all_gather(x, axis).sum(0)  24.6 us
  transfers between devices with their start and end apart: 16, of which 15 were waited for; matrix products, arithmetic and copies ran while one was open for 8% of the time, Pallas kernels for 0%

commit v1 on v0

v1 whole, which is shorter than its diff:
```python
import jax
import jax.numpy as jnp
from jax import lax
from jax.experimental import pallas as pl
from jax.experimental.pallas import tpu as pltpu
from jax.sharding import Mesh
from jax.sharding import PartitionSpec as P

COL = ("col_0", "col_1")
ROW = ("row_0", "row_1")
MESH = pl.DeviceIdType.MESH
F32 = jnp.float32
BF16 = jnp.bfloat16
NORM = 268435456.0
ROWS = 8
COLS = 16
T = 6
B = 64
J = 512
U = 256
PIECE = 16
IPIECE = 8


def dev(r, c):
    return (r // 2, r % 2, c // 4, c % 4)


def push(src, dst, send_sem, recv_sem, where):
    pltpu.make_async_remote_copy(
        src_ref=src, dst_ref=dst, send_sem=send_sem, recv_sem=recv_sem,
        device_id=where, device_id_type=MESH,
    ).start()


def drain(ref, sem):
    pltpu.make_async_copy(ref, ref, sem).wait()


def nt(a, b):
    return lax.dot_general(a, b, (((1,), (1,)), ((), ())), preferred_element_type=F32)


def tn(a, b):
    return lax.dot_general(a, b, (((0,), (0,)), ((), ())), preferred_element_type=F32)


def kernel(
    w_rec, w_in, gate_pre, cells, layer_in, h_prev, top_grad,
    o_rec, o_in, o_inp,
    wraw, tmp, wk, gp, cl, li, hp, tg, dgs, acc, fac, carry,
    sb, rb, hb, sbi, rbi, gbi, gs, ps, rs,
    ld, st, rs_s, rs_r, ag_s, ag_r, ris_s, ris_r, ia_s, ia_r, gs_s, gs_r, ps_s, ps_r,
):
    r = lax.axis_index("row_0") * 2 + lax.axis_index("row_1")
    c = lax.axis_index("col_0") * 4 + lax.axis_index("col_1")
    mine = r == c // 2
    own = (c % 2) * ROWS + r

    loads = [
        (gate_pre, gp), (cells, cl), (top_grad, tg),
        (w_rec.at[1], wraw.at[2]), (w_in.at[1], wraw.at[3]),
        (w_rec.at[0], wraw.at[0]), (w_in.at[0], wraw.at[1]),
        (h_prev, hp), (layer_in, li),
    ]
    copies = [pltpu.make_async_copy(a, b, ld.at[i]) for i, (a, b) in enumerate(loads)]
    for copy in copies:
        copy.start()

    barrier = pltpu.get_barrier_semaphore()
    for i in range(1, ROWS):
        pl.semaphore_signal(barrier, inc=1, device_id=dev((r + i) % ROWS, c), device_id_type=MESH)
    for i in range(COLS):
        @pl.when(jnp.logical_or(r != c // 2, c != i))
        def _():
            pl.semaphore_signal(barrier, inc=1, device_id=dev(c // 2, i), device_id_type=MESH)

    def relayout(m):
        tmp[...] = wraw[m].astype(F32)
        for i in range(8):
            wk[m, :, pl.ds(i * 128, 128)] = tmp[pl.ds(i, J, stride=8), :].astype(BF16)

    def factors(layer, t):
        for ut in range(2):
            lanes = pl.ds(ut * 128, 128)
            gi = jax.nn.sigmoid(gp[layer, t, :, ut * 4 + 0, :])
            gf = jax.nn.sigmoid(gp[layer, t, :, ut * 4 + 1, :])
            gc = jnp.tanh(gp[layer, t, :, ut * 4 + 2, :])
            go = jax.nn.sigmoid(gp[layer, t, :, ut * 4 + 3, :])
            th = jnp.tanh(cl[layer, t + 1, :, lanes])
            fac[layer, 0, :, lanes] = go * (1.0 - th * th)
            fac[layer, 1, :, lanes] = gc * gi * (1.0 - gi)
            fac[layer, 2, :, lanes] = cl[layer, t, :, lanes] * gf * (1.0 - gf)
            fac[layer, 3, :, lanes] = gi * (1.0 - gc * gc)
            fac[layer, 4, :, lanes] = th * go * (1.0 - go)
            fac[layer, 5, :, lanes] = gf

    def cell(layer, t, hid):
        grad = carry[layer] + hid * fac[layer, 0]
        carry[layer] = grad * fac[layer, 5]
        parts = [grad * fac[layer, 1], grad * fac[layer, 2], grad * fac[layer, 3], hid * fac[layer, 4]]
        for ut in range(2):
            for k in range(4):
                dgs[layer, t, :, pl.ds((ut * 4 + k) * 128, 128)] = (
                    parts[k][:, ut * 128 : ut * 128 + 128].astype(BF16)
                )

    def scatter(src, dst, send_sem, recv_sem):
        for i in range(2 * ROWS):
            q = (r + [4, 5, 2, 3, 6, 7, 0, 1][i // 2]) % ROWS
            h = i % 2
            @pl.when(jnp.logical_or(q != r, 2 * r + h != c))
            def _():
                push(src.at[h * ROWS + q], dst.at[c], send_sem, recv_sem, dev(q, 2 * r + h))

    def scatter_wait(ref, sem):
        @pl.when(mine)
        def _():
            drain(ref.at[pl.ds(0, COLS - 1)], sem)

        @pl.when(jnp.logical_not(mine))
        def _():
            drain(ref, sem)

    def gather(src, dst, send_sem, recv_sem):
        for i in [4, 5, 2, 3, 6, 7, 1]:
            push(src, dst.at[r], send_sem, recv_sem, dev((r + i) % ROWS, c))

    def gather_wait(ref, sem):
        drain(ref.at[pl.ds(0, ROWS - 1)], sem)

    def total(ref):
        out = ref[0]
        for i in range(1, COLS):
            out = out + ref[i]
        return out

    def keep_own(src, dst):
        @pl.when(mine)
        def _():
            dst[c] = src[own]

    def weight_grads(layer, t):
        for s, left in enumerate((hp, li)):
            for i in range(4):
                prod = tn(left[layer, t], dgs[layer, t, :, pl.ds(i * 256, 256)])
                for q in range(2):
                    where = (2 * layer + s, pl.ds(2 * i + q, J, stride=8))
                    acc[where] = acc[where] + prod[:, q * 128 : q * 128 + 128]

    def input_send(d, t):
        prod = nt(dgs[0, t], wk[1])
        for h in range(2):
            sbi[d, pl.ds(h * ROWS, ROWS)] = prod[:, h * U : h * U + U].reshape(ROWS, IPIECE, U)
        keep_own(sbi.at[d], rbi.at[d])
        scatter(sbi.at[d], rbi.at[d], ris_s.at[d], ris_r.at[d])

    def input_sum(d, t):
        scatter_wait(rbi.at[d], ris_r.at[d])
        gbi[t, r] = total(rbi.at[d])
        gather(gbi.at[t, r], gbi.at[t], ia_s.at[t], ia_r.at[t])

    zero_piece = jnp.zeros((B, U), F32)
    hb[0] = jnp.zeros((ROWS, PIECE, U), F32)
    for layer in range(2):
        carry[layer] = zero_piece
    for n in range(6):
        fac[0, n] = zero_piece

    def clear(i, x):
        acc[:, pl.ds(pl.multiple_of(i * 256, 256), 256), :] = jnp.zeros((4, 256, 128), F32)
        return x

    lax.fori_loop(0, 16, clear, 0)
    copies[0].wait()
    copies[1].wait()
    copies[2].wait()
    factors(1, T - 1)
    copies[3].wait()
    relayout(2)
    copies[4].wait()
    relayout(3)

    @pl.when(mine)
    def _():
        pl.semaphore_wait(barrier, ROWS - 1 + COLS - 1)

    @pl.when(jnp.logical_not(mine))
    def _():
        pl.semaphore_wait(barrier, ROWS - 1 + COLS)

    def diagonal(d, x):
        t1 = T - 1 - d
        t0 = T - d
        cell(1, t1, hb[d, pl.ds(0, 4)].reshape(B, U) + tg[t1])
        cell(0, t0, hb[d, pl.ds(4, 4)].reshape(B, U))
        up = nt(dgs[1, t1], wk[2])
        down = nt(dgs[1, t1], wk[3])
        for h in range(2):
            sb[d, pl.ds(h * ROWS, 4)] = up[:, h * U : h * U + U].reshape(4, PIECE, U)
            sb[d, pl.ds(h * ROWS + 4, 4)] = down[:, h * U : h * U + U].reshape(4, PIECE, U)

        @pl.when(d > 0)
        def _():
            more = nt(dgs[0, t0], wk[0])
            for h in range(2):
                at = (d, pl.ds(h * ROWS + 4, 4))
                sb[at] = sb[at] + more[:, h * U : h * U + U].reshape(4, PIECE, U)

        keep_own(sb.at[d], rb.at[d])
        scatter(sb.at[d], rb.at[d], rs_s.at[d], rs_r.at[d])

        @pl.when(d == 0)
        def _():
            copies[5].wait()
            relayout(0)
            copies[6].wait()
            relayout(1)
            copies[7].wait()
            copies[8].wait()

        @pl.when(d > 0)
        def _():
            input_send(d, t0)

        factors(0, T - 1 - d)

        @pl.when(d < T - 1)
        def _():
            factors(1, T - 2 - d)

        weight_grads(1, t1)

        @pl.when(d > 0)
        def _():
            weight_grads(0, t0)

        scatter_wait(rb.at[d], rs_r.at[d])
        hb[d + 1, r] = total(rb.at[d])
        gather(hb.at[d + 1, r], hb.at[d + 1], ag_s.at[d], ag_r.at[d])

        @pl.when(d > 0)
        def _():
            input_sum(d, t0)

        gather_wait(hb.at[d + 1], ag_r.at[d])
        return x

    lax.fori_loop(0, T, diagonal, 0)

    cell(0, 0, hb[T, pl.ds(4, 4)].reshape(B, U))
    input_send(T, 0)
    weight_grads(0, 0)

    def squares(i, x):
        part = acc[:, pl.ds(pl.multiple_of(i * 256, 256), 256), :]
        return x + jnp.sum((part * part).reshape(128, 8, 128), axis=0)

    gs[r] = lax.fori_loop(0, 16, squares, jnp.zeros((8, 128), F32))
    gather(gs.at[r], gs, gs_s, gs_r)
    gather_wait(gs, gs_r)
    row_sum = gs[0]
    for i in range(1, ROWS):
        row_sum = row_sum + gs[i]
    ps[...] = row_sum

    @pl.when(mine)
    def _():
        rs[c] = row_sum

    for i in range(2 * ROWS):
        q = (r + [4, 5, 2, 3, 6, 7, 0, 1][i // 2]) % ROWS
        h = i % 2
        @pl.when(jnp.logical_or(q != r, 2 * r + h != c))
        def _():
            push(ps, rs.at[c], ps_s, ps_r, dev(q, 2 * r + h))

    input_sum(T, 0)
    scatter_wait(rs, ps_r)
    sumsq = jnp.sum(total(rs), keepdims=True)
    scale = 1.0 / jnp.maximum(jnp.sqrt(sumsq / NORM), 0.05)

    writes = []
    for m, out in enumerate((o_rec.at[0], o_in.at[0], o_rec.at[1], o_in.at[1])):
        for q in range(2):
            def finish(i, x, m=m, q=q):
                at = pl.ds(pl.multiple_of(q * 2048 + i * 256, 256), 256)
                wraw[m, at, :] = (acc[m, at, :] * scale).astype(BF16)
                return x

            lax.fori_loop(0, 8, finish, 0)
            at = pl.ds(q * 2048, 2048)
            copy = pltpu.make_async_copy(wraw.at[m, at], out.at[at], st.at[m])
            copy.start()
            writes.append(copy)

    for t in range(T - 1, -1, -1):
        gather_wait(gbi.at[t], ia_r.at[t])
    copy = pltpu.make_async_copy(gbi, o_inp, st.at[4])
    copy.start()
    writes.append(copy)

    def sent(d, x):
        scatter_wait(sb.at[d], rs_s.at[d])
        gather_wait(hb.at[d + 1], ag_s.at[d])
        scatter_wait(sbi.at[d + 1], ris_s.at[d + 1])
        gather_wait(gbi.at[d], ia_s.at[d])
        return x

    lax.fori_loop(0, T, sent, 0)
    gather_wait(gs, gs_s)
    scatter_wait(rs, ps_s)
    for m in range(4):
        drain(wraw.at[m], st.at[m])
    writes[-1].wait()


def local(w_rec, w_in, gate_pre, cells, layer_in, h_prev, top_grad):
    def tiles(w):
        lead = w.shape[:-2]
        axes = tuple(range(len(lead)))
        n = len(lead)
        return w.reshape(lead + (4, 2, 128)).transpose(axes + (n + 1, n, n + 2))

    any_space = pl.BlockSpec(memory_space=pl.ANY)
    vmem = pltpu.VMEM
    dma = pltpu.SemaphoreType.DMA
    rec, inp, igrad = pl.pallas_call(
        kernel,
        out_shape=(
            jax.ShapeDtypeStruct((2, 8 * J, 128), BF16),
            jax.ShapeDtypeStruct((2, 8 * J, 128), BF16),
            jax.ShapeDtypeStruct((T, ROWS, IPIECE, U), F32),
        ),
        in_specs=[any_space] * 7,
        out_specs=(any_space,) * 3,
        scratch_shapes=[
            vmem((4, 8 * J, 128), BF16),
            vmem((8 * J, 128), F32),
            vmem((4, J, 4 * U), BF16),
            vmem((2, T, B, 8, 128), F32),
            vmem((2, T + 1, B, U), F32),
            vmem((2, T, B, J), BF16),
            vmem((2, T, B, J), BF16),
            vmem((T, B, U), F32),
            vmem((2, T + 1, B, 4 * U), BF16),
            vmem((4, 8 * J, 128), F32),
            vmem((2, 6, B, U), F32),
            vmem((2, B, U), F32),
            vmem((T, 2 * ROWS, PIECE, U), F32),
            vmem((T, COLS, PIECE, U), F32),
            vmem((T + 1, ROWS, PIECE, U), F32),
            vmem((T + 1, 2 * ROWS, IPIECE, U), F32),
            vmem((T + 1, COLS, IPIECE, U), F32),
            vmem((T, ROWS, IPIECE, U), F32),
            vmem((ROWS, 8, 128), F32),
            vmem((8, 128), F32),
            vmem((COLS, 8, 128), F32),
            dma((9,)), dma((5,)),
            dma((T,)), dma((T,)), dma((T,)), dma((T,)),
            dma((T + 1,)), dma((T + 1,)), dma((T,)), dma((T,)),
            dma, dma, dma, dma,
        ],
        compiler_params=pltpu.CompilerParams(
            collective_id=0, has_side_effects=True, vmem_limit_bytes=60 * 1024 * 1024
        ),
    )(
        tiles(w_rec).reshape(2, 8 * J, 128),
        tiles(w_in).reshape(2, 8 * J, 128),
        tiles(gate_pre).reshape(2, T, B, 8, 128),
        cells, layer_in, h_prev, top_grad,
    )

    def back(w):
        return w.reshape(2, J, 2, 4, 128).transpose(0, 1, 3, 2, 4).reshape(2, J, 4, U)

    return back(rec), back(inp), igrad.reshape(T, B, U)


def solution(mesh):
    torus = Mesh(mesh.devices.reshape(4, 2, 4, 4), ("row_0", "row_1", "col_0", "col_1"))
    placed = (
        P(None, ROW, None, COL),
        P(None, ROW, None, COL),
        P(None, None, None, None, COL),
        P(None, None, None, COL),
        P(None, None, None, ROW),
        P(None, None, None, ROW),
        P(None, None, COL),
    )
    return jax.shard_map(
        local,
        mesh=torus,
        in_specs=placed,
        out_specs=(P(None, ROW, None, COL), P(None, ROW, None, COL), P(None, None, COL)),
        check_vma=False,
    )
```

time: 917 us -> 107 us (0.12)
  waiting for transfers between devices: 650 us -> 0 us
  other arithmetic: 102 us -> 0 us
  Pallas kernels: 0 us -> 101 us
  local copies, waits for them, and re-layouts: 82.5 us -> 5.85 us
  blocking collectives: 32.6 us -> 0 us
  matrix products: 21.7 us -> 0 us
  between operations: 18.6 us -> 0.65 us
    all_gather x15 -> x0, waiting for transfers between devices: 565 us -> none  [the longest x7 431 us: total_of_pieces(): return lax.all_gather(x, axis).sum(0)]
    pallas_call x0 -> x1, Pallas kernels: none -> 101 us  [local(): pl.pallas_call(kernel, out_shape=(jax.ShapeDtypeStruct((2, 8 * J, 128), B...]
    psum x1 -> x0, waiting for transfers between devices: 85 us -> none  [input_units(): piece, root = own_block(lax.psum(partial_value, COL))]
    another operation x39 -> x0, other arithmetic: 46.2 us -> none
    psum x4 -> x0, blocking collectives: 32.6 us -> none  [by_axis(): x = lax.psum(x, axis)]
    select_n x21 -> x0, other arithmetic: 25.2 us -> none  [the longest x7 13.4 us: diagonal_step(): cell_next = jnp.where(valid, cell_next, jnp.zeros_like(cell_next))]
    reduce_sum x7 -> x0, other arithmetic: 24.6 us -> none  [total_of_pieces(): return lax.all_gather(x, axis).sum(0)]
    dynamic_slice x23 -> x0, local copies, waits for them, and re-layouts: 21.8 us -> none  [the longest x14 13.4 us: diagonal_step(): lax.dynamic_index_in_dim(stores[layer], clamped, 0, keepdims=False)]
  transfers between devices with their start and end apart: 16 -> 0, of which waited for: 15 -> 0; matrix products, arithmetic and copies ran while one was open for 8% -> 0% of each run, Pallas kernels for 0% -> 0%
where the time goes in v1:
time: 107 us
  Pallas kernels  101 us (94%)
  local copies, waits for them, and re-layouts  5.85 us (5%)
    pallas_call x1, Pallas kernels, local(): pl.pallas_call(kernel, out_shape=(jax.ShapeDtypeStruct((2, 8 * J, 128), B...  101 us
    unnamed x7, local copies, waits for them, and re-layouts  5.85 us

profile of v1, /device:TPU:1, one launch (start us, length us, event | category | flops | bytes accessed | tf_op | source)
XLA Modules:
  0.0 107.0 jit_solution(16881779874574484170)
XLA Ops:
  0.6 100.5 %shard_map.94 = (bf16[2,4096,128]{2,1,0:T(8,128)(2,1)}, bf16[2,4096,128]{2,1,0:T(8,128)(2,1)}, f32[6,8,8,256]{3,2,1,0:T(8,128)}) custom-call(bf16[2,4096,128]{2,1,0:T(8,128)(2,1)} %bitcast.27, bf16[2,4096,128]{2,1,0:T(8,128)(2,1)} %bitcast.28, f32[2,6,64,8,128]{4,3,2,1,0:T(8,128)} %bitcast.26, f32[2,7,64,256]{3,2,1,0:T(8,128)} %cells.1, ...), custom_call_target="tpu_custom_call" | custom-call | tf_op jit(solution)/shard_map/pallas_call | solution.py:328
  101.1 0.0 copy-start
  101.2 3.8 %copy.18 = bf16[2,512,4,256]{3,2,1,0:T(4,128)(2,1)} copy(bf16[2,512,4,256]{3,2,1,0:T(4,128)(2,1)} %bitcast.30) | data formatting | bytes 4194304
  104.9 0.0 copy-done
  104.9 0.0 copy-start.1
  104.9 1.3 %copy.19 = bf16[2,512,4,256]{3,2,1,0:T(4,128)(2,1)} copy(bf16[2,512,4,256]{3,2,1,0:T(4,128)(2,1)S(1)} %bitcast.29) | data formatting | bytes 4194304
  106.3 0.0 copy-done.1
  106.3 0.7 copy.20
Async XLA Ops:
  101.1 3.8 %copy-start = (bf16[2,4096,128]{2,1,0:T(8,128)(2,1)S(1)}, bf16[2,4096,128]{2,1,0:T(8,128)(2,1)}, u32[]{:S(2)}) copy-start(bf16[2,4096,128]{2,1,0:T(8,128)(2,1)} %get-tuple-element.7) | copy-start | bytes 6291460
  104.9 1.3 %copy-start.1 = (f32[6,8,8,256]{3,2,1,0:T(8,128)S(1)}, f32[6,8,8,256]{3,2,1,0:T(8,128)}, u32[]{:S(2)}) copy-start(f32[6,8,8,256]{3,2,1,0:T(8,128)} %get-tuple-element.8) | copy-start | bytes 1179652

commit v2 on v1

v2 whole, which is shorter than its diff:
```python
import jax
import jax.numpy as jnp
from jax import lax
from jax.experimental import pallas as pl
from jax.experimental.pallas import tpu as pltpu
from jax.sharding import Mesh
from jax.sharding import PartitionSpec as P

COL = ("col_0", "col_1")
ROW = ("row_0", "row_1")
MESH = pl.DeviceIdType.MESH
F32 = jnp.float32
BF16 = jnp.bfloat16
NORM = 268435456.0
ROWS = 8
COLS = 16
T = 6
B = 64
J = 512
U = 256
VMEM_LIMIT = 44 * 1024 * 1024
PIECE = 8


def dev(r, c):
    return (r // 2, r % 2, c // 4, c % 4)


def push(src, dst, send_sem, recv_sem, where):
    pltpu.make_async_remote_copy(
        src_ref=src, dst_ref=dst, send_sem=send_sem, recv_sem=recv_sem,
        device_id=where, device_id_type=MESH,
    ).start()


def drain(ref, sem):
    pltpu.make_async_copy(ref, ref, sem).wait()


def nt(a, b):
    return lax.dot_general(a, b, (((1,), (1,)), ((), ())), preferred_element_type=F32)


def tn(a, b):
    return lax.dot_general(a, b, (((0,), (0,)), ((), ())), preferred_element_type=F32)


def kernel(
    w_rec, w_in, gate_pre, cells, layer_in, h_prev, top_grad,
    a_rec, a_in, o_inp, o_scale,
    wraw, tmp, wk, gp, cl, li, hp, tg, dgs, fac, carry, sq,
    sb, rb, hb, gs, ps, rs,
    ld, rs_s, rs_r, ag_s, ag_r, gs_s, gs_r, ps_s, ps_r,
):
    r = lax.axis_index("row_0") * 2 + lax.axis_index("row_1")
    c = lax.axis_index("col_0") * 4 + lax.axis_index("col_1")
    mine = r == c // 2
    own = (c % 2) * ROWS + r
    grads = (a_rec, a_in)

    barrier = pltpu.get_barrier_semaphore()
    for i in range(1, ROWS):
        pl.semaphore_signal(barrier, inc=1, device_id=dev((r + i) % ROWS, c), device_id_type=MESH)
    for i in range(COLS):
        @pl.when(jnp.logical_or(r != c // 2, c != i))
        def _():
            pl.semaphore_signal(barrier, inc=1, device_id=dev(c // 2, i), device_id_type=MESH)

    last = pl.ds(T - 1, 1)
    rest = pl.ds(0, T - 1)
    loads = [
        (gate_pre.at[1, last], gp.at[1, last]), (cells.at[1], cl.at[1]), (w_rec.at[1], wraw.at[2]),
        (top_grad, tg), (w_in.at[1], wraw.at[3]),
        (w_rec.at[0], wraw.at[0]), (w_in.at[0], wraw.at[1]),
        (gate_pre.at[0], gp.at[0]), (gate_pre.at[1, rest], gp.at[1, rest]), (cells.at[0], cl.at[0]),
        (h_prev, hp), (layer_in, li),
    ]
    copies = [pltpu.make_async_copy(p, q, ld.at[i]) for i, (p, q) in enumerate(loads)]
    for copy in copies:
        copy.start()

    def relayout(m):
        tmp[...] = wraw[m].astype(F32)
        for i in range(8):
            wk[m, :, pl.ds(i * 128, 128)] = tmp[pl.ds(i, J, stride=8), :].astype(BF16)

    def factors(layer, t):
        for ut in range(2):
            lanes = pl.ds(ut * 128, 128)
            gi = jax.nn.sigmoid(gp[layer, t, :, ut * 4 + 0, :])
            gf = jax.nn.sigmoid(gp[layer, t, :, ut * 4 + 1, :])
            gc = jnp.tanh(gp[layer, t, :, ut * 4 + 2, :])
            go = jax.nn.sigmoid(gp[layer, t, :, ut * 4 + 3, :])
            th = jnp.tanh(cl[layer, t + 1, :, lanes])
            fac[layer, 0, :, lanes] = go * (1.0 - th * th)
            fac[layer, 1, :, lanes] = gc * gi * (1.0 - gi)
            fac[layer, 2, :, lanes] = cl[layer, t, :, lanes] * gf * (1.0 - gf)
            fac[layer, 3, :, lanes] = gi * (1.0 - gc * gc)
            fac[layer, 4, :, lanes] = th * go * (1.0 - go)
            fac[layer, 5, :, lanes] = gf

    def cell(layer, t, hid):
        grad = carry[layer] + hid * fac[layer, 0]
        carry[layer] = grad * fac[layer, 5]
        parts = [grad * fac[layer, 1], grad * fac[layer, 2], grad * fac[layer, 3], hid * fac[layer, 4]]
        for ut in range(2):
            for k in range(4):
                dgs[layer, t, :, pl.ds((ut * 4 + k) * 128, 128)] = (
                    parts[k][:, ut * 128 : ut * 128 + 128].astype(BF16)
                )

    def to_each(send):
        for i in range(2 * ROWS):
            q = (r + [4, 5, 2, 3, 6, 7, 0, 1][i // 2]) % ROWS
            h = i % 2
            @pl.when(jnp.logical_or(q != r, 2 * r + h != c))
            def _():
                send(h * ROWS + q, dev(q, 2 * r + h))

    def scatter(ch, s):
        @pl.when(mine)
        def _():
            rb[ch, s, c] = sb[ch, s, own]

        to_each(lambda piece, where: push(
            sb.at[ch, s, piece], rb.at[ch, s, c], rs_s.at[ch, s], rs_r.at[ch, s], where))

    def scatter_wait(ref, sem):
        @pl.when(mine)
        def _():
            drain(ref.at[pl.ds(0, COLS - 1)], sem)

        @pl.when(jnp.logical_not(mine))
        def _():
            drain(ref, sem)

    def gather(src, dst, send_sem, recv_sem):
        for i in [4, 5, 2, 3, 6, 7, 1]:
            push(src, dst.at[r], send_sem, recv_sem, dev((r + i) % ROWS, c))

    def gather_wait(ref, sem):
        drain(ref.at[pl.ds(0, ROWS - 1)], sem)

    def total(ref):
        terms = [ref[i] for i in range(COLS)]
        while len(terms) > 1:
            terms = [p + q for p, q in zip(terms[::2], terms[1::2])]
        return terms[0]

    def pass_on(ch, s, to):
        scatter_wait(rb.at[ch, s], rs_r.at[ch, s])
        hb[ch, to, r] = total(rb.at[ch, s])
        gather(hb.at[ch, to, r], hb.at[ch, to], ag_s.at[ch, to], ag_r.at[ch, to])

    def store(ch, s, prod, add=False):
        for h in range(2):
            at = (ch, s, pl.ds(h * ROWS, ROWS))
            piece = prod[:, h * U : h * U + U].reshape(ROWS, PIECE, U)
            sb[at] = sb[at] + piece if add else piece

    def folded(x):
        return jnp.sum(x.reshape(-1, 64, 128), axis=0)

    def weight_grads(layer, t, square=False):
        for s, left in enumerate((hp, li)):
            for i in range(4):
                prod = tn(left[layer, t], dgs[layer, t, :, pl.ds(i * 256, 256)])
                for q in range(2):
                    where = (layer, pl.ds(2 * i + q, J, stride=8))
                    full = grads[s][where] + prod[:, q * 128 : q * 128 + 128]
                    grads[s][where] = full
                    if square:
                        sq[...] = sq[...] + folded(full * full)

    def hidden(ch, d):
        return hb[ch, d].reshape(B, U)

    copies[0].wait()
    copies[1].wait()
    factors(1, T - 1)
    copies[2].wait()
    relayout(2)
    copies[3].wait()
    copies[4].wait()
    relayout(3)
    zero = jnp.zeros((B, U), F32)
    for layer in range(2):
        carry[layer] = zero
        hb[layer, 0] = jnp.zeros((ROWS, PIECE, U), F32)
    for n in range(6):
        fac[0, n] = zero

    @pl.when(mine)
    def _():
        pl.semaphore_wait(barrier, ROWS - 1 + COLS - 1)

    @pl.when(jnp.logical_not(mine))
    def _():
        pl.semaphore_wait(barrier, ROWS - 1 + COLS)

    def diagonal(d, x):
        t1 = T - 1 - d
        t0 = T - d

        @pl.when(d > 0)
        def _():
            gather_wait(hb.at[0, d], ag_r.at[0, d])

        cell(1, t1, hidden(0, d) + tg[t1])

        @pl.when(d < T - 1)
        def _():
            store(0, d, nt(dgs[1, t1], wk[2]))
            scatter(0, d)

        store(1, d, nt(dgs[1, t1], wk[3]))

        @pl.when(d > 0)
        def _():
            gather_wait(hb.at[1, d], ag_r.at[1, d])

        cell(0, t0, hidden(1, d))

        @pl.when(d > 0)
        def _():
            store(1, d, nt(dgs[0, t0], wk[0]), add=True)

        scatter(1, d)

        @pl.when(d == 0)
        def _():
            for n in range(2):
                for i in range(8):
                    for layer in range(2):
                        grads[n][layer, pl.ds(i * J, J), :] = jnp.zeros((J, 128), F32)
            copies[5].wait()
            relayout(0)
            copies[6].wait()
            relayout(1)
            for copy in copies[7:]:
                copy.wait()

        factors(0, T - 1 - d)

        @pl.when(d < T - 1)
        def _():
            factors(1, T - 2 - d)

        weight_grads(1, t1)

        @pl.when(d > 0)
        def _():
            store(2, t0, nt(dgs[0, t0], wk[1]))

        @pl.when(d < T - 1)
        def _():
            pass_on(0, d, d + 1)

        pass_on(1, d, d + 1)

        @pl.when(d > 0)
        def _():
            scatter(2, t0)

        @pl.when(d > 0)
        def _():
            weight_grads(0, t0)

        @pl.when(d > 1)
        def _():
            pass_on(2, t0 + 1, t0 + 1)

        return x

    lax.fori_loop(0, T, diagonal, 0)

    def squares(i, x):
        at = pl.ds(pl.multiple_of(i * 512, 512), 512)
        for n in range(2):
            part = grads[n][1, at, :]
            x = x + folded(part * part)
        return x

    sq[...] = lax.fori_loop(0, 8, squares, jnp.zeros((64, 128), F32))
    gather_wait(hb.at[1, T], ag_r.at[1, T])
    cell(0, 0, hidden(1, T))
    store(2, 0, nt(dgs[0, 0], wk[1]))
    scatter(2, 0)
    weight_grads(0, 0, square=True)
    gs[r] = jnp.sum(sq[...].reshape(8, 8, 128), axis=0)
    gather(gs.at[r], gs, gs_s, gs_r)
    pass_on(2, 1, 1)
    gather_wait(gs, gs_r)
    row_sum = gs[0]
    for i in range(1, ROWS):
        row_sum = row_sum + gs[i]
    ps[...] = row_sum

    @pl.when(mine)
    def _():
        rs[c] = row_sum

    to_each(lambda piece, where: push(ps, rs.at[c], ps_s, ps_r, where))
    pass_on(2, 0, 0)
    scatter_wait(rs, ps_r)
    sumsq = jnp.sum(total(rs), keepdims=True)
    scale = 1.0 / jnp.maximum(jnp.sqrt(sumsq / NORM), 0.05)
    o_scale[...] = jnp.broadcast_to(scale, (8, 128))

    def sent(d, x):
        @pl.when(d < T - 1)
        def _():
            scatter_wait(sb.at[0, d], rs_s.at[0, d])
            gather_wait(hb.at[0, d + 1], ag_s.at[0, d + 1])

        scatter_wait(sb.at[1, d], rs_s.at[1, d])
        gather_wait(hb.at[1, d + 1], ag_s.at[1, d + 1])
        scatter_wait(sb.at[2, d], rs_s.at[2, d])
        gather_wait(hb.at[2, d], ag_s.at[2, d])
        gather_wait(hb.at[2, d], ag_r.at[2, d])
        return x

    lax.fori_loop(0, T, sent, 0)
    gather_wait(gs, gs_s)
    scatter_wait(rs, ps_s)
    o_inp[...] = hb[2, pl.ds(0, T)]


def local(w_rec, w_in, gate_pre, cells, layer_in, h_prev, top_grad):
    def tiles(w):
        lead = w.shape[:-2]
        axes = tuple(range(len(lead)))
        n = len(lead)
        return w.reshape(lead + (4, 2, 128)).transpose(axes + (n + 1, n, n + 2))

    any_space = pl.BlockSpec(memory_space=pltpu.HBM)
    in_vmem = pl.BlockSpec(memory_space=pltpu.VMEM)
    vmem = pltpu.VMEM
    dma = pltpu.SemaphoreType.DMA
    rec, inp, igrad, scale = pl.pallas_call(
        kernel,
        out_shape=(
            vmem((2, 8 * J, 128), F32),
            vmem((2, 8 * J, 128), F32),
            vmem((T, ROWS, PIECE, U), F32),
            vmem((8, 128), F32),
        ),
        in_specs=[any_space] * 7,
        out_specs=(in_vmem,) * 4,
        scratch_shapes=[
            vmem((4, 8 * J, 128), BF16),
            vmem((8 * J, 128), F32),
            vmem((4, J, 4 * U), BF16),
            vmem((2, T, B, 8, 128), F32),
            vmem((2, T + 1, B, U), F32),
            vmem((2, T, B, J), BF16),
            vmem((2, T, B, J), BF16),
            vmem((T, B, U), F32),
            vmem((2, T + 1, B, 4 * U), BF16),
            vmem((2, 6, B, U), F32),
            vmem((2, B, U), F32),
            vmem((64, 128), F32),
            vmem((3, T, 2 * ROWS, PIECE, U), F32),
            vmem((3, T, COLS, PIECE, U), F32),
            vmem((3, T + 1, ROWS, PIECE, U), F32),
            vmem((ROWS, 8, 128), F32),
            vmem((8, 128), F32),
            vmem((COLS, 8, 128), F32),
            dma((12,)),
            dma((3, T)), dma((3, T)), dma((3, T + 1)), dma((3, T + 1)),
            dma, dma, dma, dma,
        ],
        compiler_params=pltpu.CompilerParams(
            collective_id=0, has_side_effects=True, vmem_limit_bytes=VMEM_LIMIT
        ),
    )(*[pltpu.with_memory_space_constraint(x, pltpu.HBM) for x in (
        tiles(w_rec).reshape(2, 8 * J, 128),
        tiles(w_in).reshape(2, 8 * J, 128),
        tiles(gate_pre).reshape(2, T, B, 8, 128),
        cells, layer_in, h_prev, top_grad,
    )])

    def back(w):
        w = (w * scale[0, 0]).astype(BF16)
        return w.reshape(2, J, 2, 4, 128).transpose(0, 1, 3, 2, 4).reshape(2, J, 4, U)

    return back(rec), back(inp), igrad.reshape(T, B, U)


def solution(mesh):
    torus = Mesh(mesh.devices.reshape(4, 2, 4, 4), ("row_0", "row_1", "col_0", "col_1"))
    placed = (
        P(None, ROW, None, COL),
        P(None, ROW, None, COL),
        P(None, None, None, None, COL),
        P(None, None, None, COL),
        P(None, None, None, ROW),
        P(None, None, None, ROW),
        P(None, None, COL),
    )
    return jax.shard_map(
        local,
        mesh=torus,
        in_specs=placed,
        out_specs=(P(None, ROW, None, COL), P(None, ROW, None, COL), P(None, None, COL)),
        check_vma=False,
    )
```

time: 107 us -> 87.5 us (0.82)
  Pallas kernels: 101 us -> 82.2 us
  local copies, waits for them, and re-layouts: 5.85 us -> 1.26 us
  other arithmetic: 0 us -> 3.3 us
    pallas_call x1, Pallas kernels: 101 us -> 82.2 us  [local(): pl.pallas_call(kernel, out_shape=(vmem((2, 8 * J, 128), F32), vmem((2, 8...]
    unnamed x7 -> x1, local copies, waits for them, and re-layouts: 5.85 us -> 0.75 us
    convert_element_type x0 -> x1, other arithmetic: none -> 3.3 us  [back(): w = (w * scale[0, 0]).astype(BF16)]
where the time goes in v2:
time: 87.5 us; the launch traced here: 87.4 us
  Pallas kernels  82.2 us (94%)
  other arithmetic  3.3 us (4%)
  local copies, waits for them, and re-layouts  1.26 us (1%)
    pallas_call x1, Pallas kernels, local(): pl.pallas_call(kernel, out_shape=(vmem((2, 8 * J, 128), F32), vmem((2, 8...  82.2 us
    convert_element_type x1, other arithmetic, back(): w = (w * scale[0, 0]).astype(BF16)  3.3 us

profile of v2, /device:TPU:1, one launch (start us, length us, event | category | flops | bytes accessed | tf_op | source)
XLA Modules:
  0.0 87.4 jit_solution(5903174824749642858)
XLA Ops:
  0.6 82.2 %shard_map.94 = (f32[2,4096,128]{2,1,0:T(8,128)S(1)}, f32[2,4096,128]{2,1,0:T(8,128)S(1)}, f32[6,8,8,256]{3,2,1,0:T(8,128)S(1)}, f32[8,128]{1,0:T(8,128)S(1)}) custom-call(bf16[2,4096,128]{2,1,0:T(8,128)(2,1)} %bitcast.29, bf16[2,4096,128]{2,1,0:T(8,128)(2,1)} %bitcast.30, f32[2,6,64,8,128]{4,3,2,1,0:T(8,128)} %bitcast.28, f32[2,7,64,256]{3,2,1,0:T(8,128)} %cells.1, ...), custom_call_target="tpu_custom_call" | custom-call | tf_op jit(solution)/shard_map/pallas_call | solution.py:340
  82.8 0.5 slice.4
  83.4 3.3 %multiply_convert_fusion = (bf16[2,4096,128]{2,1,0:T(8,128)(2,1)}, bf16[2,4096,128]{2,1,0:T(8,128)(2,1)}) fusion(f32[2,4096,128]{2,1,0:T(8,128)S(1)} %get-tuple-element.9, f32[]{:T(128)} %bitcast.9, f32[2,4096,128]{2,1,0:T(8,128)S(1)} %get-tuple-element.7), kind=kLoop, calls=%fused_computation | loop fusion | flops 4194304 | bytes 12582916 | tf_op jit(solution)/shard_map/convert_element_type | solution.py:384
  86.7 0.7 copy.16

commit v3 on v2

v3 whole, which is shorter than its diff:
```python
import jax
import jax.numpy as jnp
from jax import lax
from jax.experimental import pallas as pl
from jax.experimental.pallas import tpu as pltpu
from jax.sharding import Mesh
from jax.sharding import PartitionSpec as P

COL = ("col_0", "col_1")
ROW = ("row_0", "row_1")
MESH = pl.DeviceIdType.MESH
F32 = jnp.float32
BF16 = jnp.bfloat16
NORM = 268435456.0
ROWS = 8
COLS = 16
T = 6
B = 64
J = 512
U = 256
VMEM_LIMIT = 50 * 1024 * 1024
OWNERS = 4
PIECE = 16


def dev(r, c):
    return (r // 2, r % 2, c // 4, c % 4)


def push(src, dst, send_sem, recv_sem, where):
    pltpu.make_async_remote_copy(
        src_ref=src, dst_ref=dst, send_sem=send_sem, recv_sem=recv_sem,
        device_id=where, device_id_type=MESH,
    ).start()


def drain(ref, sem):
    pltpu.make_async_copy(ref, ref, sem).wait()


def nn(a, b):
    return jnp.dot(a, b, preferred_element_type=F32)


def tn(a, b):
    return lax.dot_general(a, b, (((0,), (0,)), ((), ())), preferred_element_type=F32)


def kernel(
    w_rec, w_in, gate_pre, cells, layer_in, h_prev, top_grad,
    o_rec, o_in, o_inp,
    wraw, tmp, wk, gp, cl, li, hp, tg, dgs, a_rec, a_in, fac, carry, sq,
    sb, rb, hb, parts,
    ld, rs_s, rs_r, ag_s, ag_r, ps_s, ps_r,
):
    x = lax.axis_index("row_0")
    k = lax.axis_index("row_1")
    r = x * 2 + k
    y = lax.axis_index("col_0")
    z = lax.axis_index("col_1")
    c = y * 4 + z
    me = r * COLS + c
    owner = k == 1
    mine = jnp.logical_and(owner, r == c // 2)
    own = (c % 2) * OWNERS + x
    grads = (a_rec, a_in)

    barrier = pltpu.get_barrier_semaphore()
    for i in range(OWNERS):
        @pl.when(2 * i + 1 != r)
        def _():
            pl.semaphore_signal(barrier, inc=1, device_id=dev(2 * i + 1, c), device_id_type=MESH)

    for i in range(COLS):
        @pl.when(jnp.logical_and(owner, jnp.logical_or(r != c // 2, c != i)))
        def _():
            pl.semaphore_signal(barrier, inc=1, device_id=dev(c // 2, i), device_id_type=MESH)

    last = pl.ds(T - 1, 1)
    rest = pl.ds(0, T - 1)
    loads = [
        (gate_pre.at[1, last], gp.at[1, last]), (cells.at[1], cl.at[1]), (w_rec.at[1], wraw.at[2]),
        (top_grad, tg), (w_in.at[1], wraw.at[3]),
        (w_rec.at[0], wraw.at[0]), (w_in.at[0], wraw.at[1]),
        (gate_pre.at[0], gp.at[0]), (gate_pre.at[1, rest], gp.at[1, rest]), (cells.at[0], cl.at[0]),
        (h_prev, hp), (layer_in, li),
    ]
    copies = [pltpu.make_async_copy(p, q, ld.at[i]) for i, (p, q) in enumerate(loads)]
    for copy in copies:
        copy.start()

    def relayout(m):
        tmp[...] = wraw[m].astype(F32)
        for i in range(8):
            wk[m, pl.ds(i * 128, 128), :] = tmp[pl.ds(i, J, stride=8), :].T.astype(BF16)

    def factors(layer, t):
        for ut in range(2):
            lanes = pl.ds(ut * 128, 128)
            gi = jax.nn.sigmoid(gp[layer, t, :, ut * 4 + 0, :])
            gf = jax.nn.sigmoid(gp[layer, t, :, ut * 4 + 1, :])
            gc = jnp.tanh(gp[layer, t, :, ut * 4 + 2, :])
            go = jax.nn.sigmoid(gp[layer, t, :, ut * 4 + 3, :])
            th = jnp.tanh(cl[layer, t + 1, :, lanes])
            fac[layer, 0, :, lanes] = go * (1.0 - th * th)
            fac[layer, 1, :, lanes] = gc * gi * (1.0 - gi)
            fac[layer, 2, :, lanes] = cl[layer, t, :, lanes] * gf * (1.0 - gf)
            fac[layer, 3, :, lanes] = gi * (1.0 - gc * gc)
            fac[layer, 4, :, lanes] = th * go * (1.0 - go)
            fac[layer, 5, :, lanes] = gf

    def cell(layer, t, hid):
        grad = carry[layer] + hid * fac[layer, 0]
        carry[layer] = grad * fac[layer, 5]
        parts = [grad * fac[layer, 1], grad * fac[layer, 2], grad * fac[layer, 3], hid * fac[layer, 4]]
        for ut in range(2):
            for k in range(4):
                dgs[layer, t, :, pl.ds((ut * 4 + k) * 128, 128)] = (
                    parts[k][:, ut * 128 : ut * 128 + 128].astype(BF16)
                )

    def scatter(ch, s):
        @pl.when(mine)
        def _():
            rb[ch, s, c] = sb[ch, s, own]

        for i in range(2 * OWNERS):
            q = (x + [2, 1, 3, 0][i // 2]) % OWNERS
            h = i % 2
            @pl.when(jnp.logical_or(2 * q + 1 != r, 2 * r + h != c))
            def _():
                push(sb.at[ch, s, h * OWNERS + q], rb.at[ch, s, c], rs_s.at[ch, s], rs_r.at[ch, s],
                     dev(2 * q + 1, 2 * r + h))

    def scatter_sent(ch, s):
        @pl.when(mine)
        def _():
            drain(sb.at[ch, s, pl.ds(0, 2 * OWNERS - 1)], rs_s.at[ch, s])

        @pl.when(jnp.logical_not(mine))
        def _():
            drain(sb.at[ch, s], rs_s.at[ch, s])

    def gather_wait(ch, s):
        @pl.when(owner)
        def _():
            drain(hb.at[ch, s, pl.ds(0, OWNERS - 1)], ag_r.at[ch, s])

        @pl.when(jnp.logical_not(owner))
        def _():
            drain(hb.at[ch, s], ag_r.at[ch, s])

    def gather_sent(ch, s):
        @pl.when(owner)
        def _():
            drain(rb.at[0, 0, pl.ds(0, ROWS - 1)], ag_s.at[ch, s])

    def tree(terms):
        while len(terms) > 1:
            terms = [p + q for p, q in zip(terms[::2], terms[1::2])]
        return terms[0]

    def pass_on(ch, s, to):
        @pl.when(mine)
        def _():
            drain(rb.at[ch, s, pl.ds(0, COLS - 1)], rs_r.at[ch, s])

        @pl.when(jnp.logical_and(owner, jnp.logical_not(mine)))
        def _():
            drain(rb.at[ch, s], rs_r.at[ch, s])

        @pl.when(owner)
        def _():
            hb[ch, to, x] = tree([rb[ch, s, i] for i in range(COLS)])
            for i in [4, 5, 2, 3, 6, 7, 1]:
                at = (x + i // 2) % OWNERS * 2 + (1 + i) % 2
                push(hb.at[ch, to, x], hb.at[ch, to, x], ag_s.at[ch, to], ag_r.at[ch, to], dev(at, c))

    def store(ch, s, prod, add=False):
        for h in range(2):
            at = (ch, s, pl.ds(h * OWNERS, OWNERS))
            piece = prod[:, h * U : h * U + U].reshape(OWNERS, PIECE, U)
            sb[at] = sb[at] + piece if add else piece

    def folded(x):
        return jnp.sum(x.reshape(-1, 64, 128), axis=0)

    def weight_grads(layer, t, square=False):
        two = pl.ds(t, 2)
        for s, left in enumerate((hp, li)):
            for i in range(4):
                prod = tn(left[layer, two].reshape(2 * B, J),
                          dgs[layer, two, :, pl.ds(i * 256, 256)].reshape(2 * B, 256))
                for q in range(2):
                    where = (layer, pl.ds(2 * i + q, J, stride=8))
                    full = grads[s][where] + prod[:, q * 128 : q * 128 + 128]
                    grads[s][where] = full
                    if square:
                        sq[...] = sq[...] + folded(full * full)

    def hidden(ch, d):
        return hb[ch, d].reshape(B, U)

    copies[0].wait()
    copies[1].wait()
    factors(1, T - 1)
    copies[2].wait()
    relayout(2)
    copies[3].wait()
    zero = jnp.zeros((B, U), F32)
    for layer in range(2):
        carry[layer] = zero
        hb[layer, 0] = jnp.zeros((OWNERS, PIECE, U), F32)
    for n in range(6):
        fac[0, n] = zero

    @pl.when(mine)
    def _():
        pl.semaphore_wait(barrier, ROWS - 1 + 2 * OWNERS - 1)

    @pl.when(jnp.logical_and(owner, jnp.logical_not(mine)))
    def _():
        pl.semaphore_wait(barrier, ROWS - 1 + 2 * OWNERS)

    @pl.when(jnp.logical_not(owner))
    def _():
        pl.semaphore_wait(barrier, 2 * OWNERS)

    def diagonal(d, _):
        t1 = T - 1 - d
        t0 = T - d

        @pl.when(d > 0)
        def _():
            gather_wait(0, d)

        cell(1, t1, hidden(0, d) + tg[t1])

        @pl.when(d < T - 1)
        def _():
            store(0, d, nn(dgs[1, t1], wk[2]))
            scatter(0, d)

        @pl.when(d == 0)
        def _():
            copies[4].wait()
            relayout(3)

        store(1, d, nn(dgs[1, t1], wk[3]))

        @pl.when(d > 0)
        def _():
            gather_wait(1, d)

        cell(0, t0, hidden(1, d))

        @pl.when(d > 0)
        def _():
            store(1, d, nn(dgs[0, t0], wk[0]), add=True)

        scatter(1, d)

        @pl.when(d == 0)
        def _():
            for n in range(2):
                for i in range(8):
                    for layer in range(2):
                        grads[n][layer, pl.ds(i * J, J), :] = jnp.zeros((J, 128), F32)
            copies[5].wait()
            relayout(0)
            copies[6].wait()
            relayout(1)
            for copy in copies[7:]:
                copy.wait()

        factors(0, T - 1 - d)

        @pl.when(d < T - 1)
        def _():
            factors(1, T - 2 - d)

        @pl.when(d > 0)
        def _():
            store(2, t0, nn(dgs[0, t0], wk[1]))

        @pl.when(d < T - 1)
        def _():
            pass_on(0, d, d + 1)

        pass_on(1, d, d + 1)

        @pl.when(d > 0)
        def _():
            scatter(2, t0)

        @pl.when(d % 2 == 1)
        def _():
            weight_grads(1, t1)

        @pl.when(jnp.logical_and(d > 0, d % 2 == 0))
        def _():
            weight_grads(0, t0)

        @pl.when(d > 1)
        def _():
            pass_on(2, t0 + 1, t0 + 1)

        return 0

    lax.fori_loop(0, T, diagonal, 0)

    def squares(i, x):
        at = pl.ds(pl.multiple_of(i * 512, 512), 512)
        for n in range(2):
            part = grads[n][1, at, :]
            x = x + folded(part * part)
        return x

    sq[...] = lax.fori_loop(0, 8, squares, jnp.zeros((64, 128), F32))
    gather_wait(1, T)
    cell(0, 0, hidden(1, T))
    store(2, 0, nn(dgs[0, 0], wk[1]))
    scatter(2, 0)
    weight_grads(0, 0, square=True)
    parts[me] = jnp.sum(sq[...], axis=0, keepdims=True)

    for i in (2, 1, 3, 0):
        for n in (2, 1, 3, 0):
            for m in (2, 1, 3, 0):
                for core in range(2):
                    if (i, n, m, core) != (0, 0, 0, 0):
                        there = ((x + i) % 4, (k + core) % 2, (y + n) % 4, (z + m) % 4)
                        push(parts.at[me], parts.at[me], ps_s, ps_r, there)
    pass_on(2, 1, 1)
    pass_on(2, 0, 0)
    drain(parts.at[pl.ds(0, 127)], ps_r)
    sumsq = jnp.sum(jnp.sum(parts[...], axis=0), keepdims=True)
    scale = 1.0 / jnp.maximum(jnp.sqrt(sumsq / NORM), 0.05)

    def finish(i, _):
        at = pl.ds(pl.multiple_of(i * 512, 512), 512)
        for out, full in ((o_rec, a_rec), (o_in, a_in)):
            for layer in range(2):
                out[layer, at, :] = (full[layer, at, :] * scale).astype(BF16)
        return 0

    lax.fori_loop(0, 8, finish, 0)

    def sent(d, _):
        @pl.when(d < T - 1)
        def _():
            scatter_sent(0, d)
            gather_sent(0, d + 1)

        scatter_sent(1, d)
        gather_sent(1, d + 1)
        scatter_sent(2, d)
        gather_sent(2, d)
        return 0

    lax.fori_loop(0, T, sent, 0)
    drain(parts.at[pl.ds(0, 127)], ps_s)
    for t in range(T - 1, -1, -1):
        gather_wait(2, t)
    o_inp[...] = hb[2, pl.ds(0, T)]


def flush(rec, inp, igrad, o_rec, o_in, o_igrad, sem):
    copies = []
    for src, dst in ((rec, o_rec), (inp, o_in)):
        for layer in range(2):
            for i in range(4):
                at = pl.ds(i * 1024, 1024)
                copies.append((src.at[layer, at], dst.at[layer, at]))
    copies.append((igrad, o_igrad))
    copies = [pltpu.make_async_copy(p, q, sem.at[i]) for i, (p, q) in enumerate(copies)]
    for copy in copies:
        copy.start()
    for copy in copies:
        copy.wait()


def local(w_rec, w_in, gate_pre, cells, layer_in, h_prev, top_grad):
    def tiles(w):
        lead = w.shape[:-2]
        axes = tuple(range(len(lead)))
        n = len(lead)
        return w.reshape(lead + (4, 2, 128)).transpose(axes + (n + 1, n, n + 2))

    any_space = pl.BlockSpec(memory_space=pltpu.HBM)
    in_vmem = pl.BlockSpec(memory_space=pltpu.VMEM)
    vmem = pltpu.VMEM
    dma = pltpu.SemaphoreType.DMA
    done = pl.pallas_call(
        kernel,
        out_shape=(
            vmem((2, 8 * J, 128), BF16),
            vmem((2, 8 * J, 128), BF16),
            vmem((T, OWNERS, PIECE, U), F32),
        ),
        in_specs=[any_space] * 7,
        out_specs=(in_vmem,) * 3,
        scratch_shapes=[
            vmem((4, 8 * J, 128), BF16),
            vmem((8 * J, 128), F32),
            vmem((4, 4 * U, J), BF16),
            vmem((2, T, B, 8, 128), F32),
            vmem((2, T + 1, B, U), F32),
            vmem((2, T, B, J), BF16),
            vmem((2, T, B, J), BF16),
            vmem((T, B, U), F32),
            vmem((2, T + 1, B, 4 * U), BF16),
            vmem((2, 8 * J, 128), F32),
            vmem((2, 8 * J, 128), F32),
            vmem((2, 6, B, U), F32),
            vmem((2, B, U), F32),
            vmem((64, 128), F32),
            vmem((3, T, 2 * OWNERS, PIECE, U), F32),
            vmem((3, T, COLS, PIECE, U), F32),
            vmem((3, T + 1, OWNERS, PIECE, U), F32),
            vmem((ROWS * COLS, 1, 128), F32),
            dma((12,)),
            dma((3, T)), dma((3, T)), dma((3, T + 1)), dma((3, T + 1)),
            dma, dma,
        ],
        compiler_params=pltpu.CompilerParams(
            collective_id=0, has_side_effects=True, vmem_limit_bytes=VMEM_LIMIT
        ),
    )(*[pltpu.with_memory_space_constraint(x, pltpu.HBM) for x in (
        tiles(w_rec).reshape(2, 8 * J, 128),
        tiles(w_in).reshape(2, 8 * J, 128),
        tiles(gate_pre).reshape(2, T, B, 8, 128),
        cells, layer_in, h_prev, top_grad,
    )])

    rec, inp, igrad = pl.pallas_call(
        flush,
        out_shape=tuple(jax.ShapeDtypeStruct(x.shape, x.dtype) for x in done),
        in_specs=[in_vmem] * 3,
        out_specs=(any_space,) * 3,
        scratch_shapes=[dma((17,))],
        compiler_params=pltpu.CompilerParams(vmem_limit_bytes=8 * 1024 * 1024),
    )(*[pltpu.with_memory_space_constraint(x, pltpu.VMEM) for x in done])

    def back(w):
        return w.reshape(2, J, 2, 4, 128).transpose(0, 1, 3, 2, 4).reshape(2, J, 4, U)

    return back(rec), back(inp), igrad.reshape(T, B, U)


def solution(mesh):
    torus = Mesh(mesh.devices.reshape(4, 2, 4, 4), ("row_0", "row_1", "col_0", "col_1"))
    placed = (
        P(None, ROW, None, COL),
        P(None, ROW, None, COL),
        P(None, None, None, None, COL),
        P(None, None, None, COL),
        P(None, None, None, ROW),
        P(None, None, None, ROW),
        P(None, None, COL),
    )
    return jax.shard_map(
        local,
        mesh=torus,
        in_specs=placed,
        out_specs=(P(None, ROW, None, COL), P(None, ROW, None, COL), P(None, None, COL)),
        check_vma=False,
    )
```

time: 87.5 us -> 79.7 us (0.911)
  other arithmetic: 3.3 us -> 0 us
  Pallas kernels: 82.2 us -> 78.9 us
  local copies, waits for them, and re-layouts: 1.26 us -> 0 us
    convert_element_type x1 -> x0, other arithmetic: 3.3 us -> none  [back(): w = (w * scale[0, 0]).astype(BF16)]
    pallas_call x1 -> x2, Pallas kernels: 82.2 us -> 78.9 us  [the longest x1 76.7 us: local(): pl.pallas_call(kernel, out_shape=(vmem((2, 8 * J, 128), BF16), vmem((2, 8...]
where the time goes in v3:
time: 79.7 us; the launch traced here: 79.6 us
  Pallas kernels  78.9 us (99%)
    pallas_call x1, Pallas kernels, local(): pl.pallas_call(kernel, out_shape=(vmem((2, 8 * J, 128), BF16), vmem((2, 8...  76.7 us
    pallas_call x1, Pallas kernels, local(): pl.pallas_call(flush, out_shape=tuple((jax.ShapeDtypeStruct(x.shape, x.dt...  2.27 us

profile of v3, /device:TPU:1, one launch (start us, length us, event | category | flops | bytes accessed | tf_op | source)
XLA Modules:
  0.0 79.6 jit_solution(16130161945163402531)
XLA Ops:
  0.6 76.7 %shard_map.94 = (bf16[2,4096,128]{2,1,0:T(8,128)(2,1)S(1)}, bf16[2,4096,128]{2,1,0:T(8,128)(2,1)S(1)}, f32[6,4,16,256]{3,2,1,0:T(8,128)S(1)}) custom-call(bf16[2,4096,128]{2,1,0:T(8,128)(2,1)} %bitcast.27, bf16[2,4096,128]{2,1,0:T(8,128)(2,1)} %bitcast.28, f32[2,6,64,8,128]{4,3,2,1,0:T(8,128)} %bitcast.26, f32[2,7,64,256]{3,2,1,0:T(8,128)} %cells.1, ...), custom_call_target="tpu_custom_call" | custom-call | tf_op jit(solution)/shard_map/pallas_call | solution.py:394
  77.3 2.3 %shard_map.95 = (bf16[2,4096,128]{2,1,0:T(8,128)(2,1)}, bf16[2,4096,128]{2,1,0:T(8,128)(2,1)}, f32[6,4,16,256]{3,2,1,0:T(8,128)}) custom-call(bf16[2,4096,128]{2,1,0:T(8,128)(2,1)S(1)} %get-tuple-element.9.rec, bf16[2,4096,128]{2,1,0:T(8,128)(2,1)S(1)} %get-tuple-element.10.inp, f32[6,4,16,256]{3,2,1,0:T(8,128)S(1)} %get-tuple-element.11.igrad), custom_call_target="tpu_custom_call" | custom-call | tf_op jit(solution)/shard_map/pallas_call | solution.py:436

commit v4 on v3

--- a/solution.py
+++ b/solution.py
@@ -1,3 +1,5 @@
+import itertools
+
 import jax
 import jax.numpy as jnp
 from jax import lax
@@ -78,12 +80,13 @@
 
     last = pl.ds(T - 1, 1)
     rest = pl.ds(0, T - 1)
+    ends = pl.ds(T - 1, 2)
     loads = [
-        (gate_pre.at[1, last], gp.at[1, last]), (cells.at[1], cl.at[1]), (w_rec.at[1], wraw.at[2]),
+        (gate_pre.at[1, last], gp.at[1, last]), (cells.at[1, ends], cl.at[1, ends]), (w_rec.at[1], wraw.at[2]),
         (top_grad, tg), (w_in.at[1], wraw.at[3]),
         (w_rec.at[0], wraw.at[0]), (w_in.at[0], wraw.at[1]),
         (gate_pre.at[0], gp.at[0]), (gate_pre.at[1, rest], gp.at[1, rest]), (cells.at[0], cl.at[0]),
-        (h_prev, hp), (layer_in, li),
+        (cells.at[1, rest], cl.at[1, rest]), (h_prev, hp), (layer_in, li),
     ]
     copies = [pltpu.make_async_copy(p, q, ld.at[i]) for i, (p, q) in enumerate(loads)]
     for copy in copies:
@@ -119,14 +122,14 @@
                     parts[k][:, ut * 128 : ut * 128 + 128].astype(BF16)
                 )
 
-    def scatter(ch, s):
-        @pl.when(mine)
-        def _():
-            rb[ch, s, c] = sb[ch, s, own]
-
-        for i in range(2 * OWNERS):
-            q = (x + [2, 1, 3, 0][i // 2]) % OWNERS
-            h = i % 2
+    def scatter(ch, s, halves=(0, 1)):
+        if 1 in halves:
+            @pl.when(mine)
+            def _():
+                rb[ch, s, c] = sb[ch, s, own]
+
+        for i, h in itertools.product((2, 1, 3, 0), halves):
+            q = (x + i) % OWNERS
             @pl.when(jnp.logical_or(2 * q + 1 != r, 2 * r + h != c))
             def _():
                 push(sb.at[ch, s, h * OWNERS + q], rb.at[ch, s, c], rs_s.at[ch, s], rs_r.at[ch, s],
@@ -176,11 +179,13 @@
                 at = (x + i // 2) % OWNERS * 2 + (1 + i) % 2
                 push(hb.at[ch, to, x], hb.at[ch, to, x], ag_s.at[ch, to], ag_r.at[ch, to], dev(at, c))
 
-    def store(ch, s, prod, add=False):
+    def store(ch, s, left, m, add=False, send=False):
         for h in range(2):
             at = (ch, s, pl.ds(h * OWNERS, OWNERS))
-            piece = prod[:, h * U : h * U + U].reshape(OWNERS, PIECE, U)
+            piece = nn(left, wk[m, :, pl.ds(h * U, U)]).reshape(OWNERS, PIECE, U)
             sb[at] = sb[at] + piece if add else piece
+            if send:
+                scatter(ch, s, (h,))
 
     def folded(x):
         return jnp.sum(x.reshape(-1, 64, 128), axis=0)
@@ -238,15 +243,14 @@
 
         @pl.when(d < T - 1)
         def _():
-            store(0, d, nn(dgs[1, t1], wk[2]))
-            scatter(0, d)
+            store(0, d, dgs[1, t1], 2, send=True)
 
         @pl.when(d == 0)
         def _():
             copies[4].wait()
             relayout(3)
 
-        store(1, d, nn(dgs[1, t1], wk[3]))
+        store(1, d, dgs[1, t1], 3)
 
         @pl.when(d > 0)
         def _():
@@ -256,9 +260,11 @@
 
         @pl.when(d > 0)
         def _():
-            store(1, d, nn(dgs[0, t0], wk[0]), add=True)
-
-        scatter(1, d)
+            store(1, d, dgs[0, t0], 0, add=True, send=True)
+
+        @pl.when(d == 0)
+        def _():
+            scatter(1, d)
 
         @pl.when(d == 0)
         def _():
@@ -281,7 +287,15 @@
 
         @pl.when(d > 0)
         def _():
-            store(2, t0, nn(dgs[0, t0], wk[1]))
+            store(2, t0, dgs[0, t0], 1)
+
+        @pl.when(d % 2 == 1)
+        def _():
+            weight_grads(1, t1)
+
+        @pl.when(jnp.logical_and(d > 0, d % 2 == 0))
+        def _():
+            weight_grads(0, t0)
 
         @pl.when(d < T - 1)
         def _():
@@ -292,14 +306,6 @@
         @pl.when(d > 0)
         def _():
             scatter(2, t0)
-
-        @pl.when(d % 2 == 1)
-        def _():
-            weight_grads(1, t1)
-
-        @pl.when(jnp.logical_and(d > 0, d % 2 == 0))
-        def _():
-            weight_grads(0, t0)
 
         @pl.when(d > 1)
         def _():
@@ -319,8 +325,7 @@
     sq[...] = lax.fori_loop(0, 8, squares, jnp.zeros((64, 128), F32))
     gather_wait(1, T)
     cell(0, 0, hidden(1, T))
-    store(2, 0, nn(dgs[0, 0], wk[1]))
-    scatter(2, 0)
+    store(2, 0, dgs[0, 0], 1, send=True)
     weight_grads(0, 0, square=True)
     parts[me] = jnp.sum(sq[...], axis=0, keepdims=True)
 
@@ -419,7 +424,7 @@
             vmem((3, T, COLS, PIECE, U), F32),
             vmem((3, T + 1, OWNERS, PIECE, U), F32),
             vmem((ROWS * COLS, 1, 128), F32),
-            dma((12,)),
+            dma((13,)),
             dma((3, T)), dma((3, T)), dma((3, T + 1)), dma((3, T + 1)),
             dma, dma,
         ],

time: 79.7 us -> 78.2 us (0.981)
  Pallas kernels: 78.9 us -> 77.5 us
    pallas_call x1, Pallas kernels: 76.7 us -> 75.2 us  [local(): pl.pallas_call(kernel, out_shape=(vmem((2, 8 * J, 128), BF16), vmem((2, 8...]
where the time goes in v4:
time: 78.2 us; the launch traced here: 78.1 us
  Pallas kernels  77.5 us (99%)
    pallas_call x1, Pallas kernels, local(): pl.pallas_call(kernel, out_shape=(vmem((2, 8 * J, 128), BF16), vmem((2, 8...  75.2 us
    pallas_call x1, Pallas kernels, local(): pl.pallas_call(flush, out_shape=tuple((jax.ShapeDtypeStruct(x.shape, x.dt...  2.27 us

profile of v4, /device:TPU:1, one launch (start us, length us, event | category | flops | bytes accessed | tf_op | source)
XLA Modules:
  0.0 78.1 jit_solution(6751809847922093525)
XLA Ops:
  0.6 75.2 %shard_map.94 = (bf16[2,4096,128]{2,1,0:T(8,128)(2,1)S(1)}, bf16[2,4096,128]{2,1,0:T(8,128)(2,1)S(1)}, f32[6,4,16,256]{3,2,1,0:T(8,128)S(1)}) custom-call(bf16[2,4096,128]{2,1,0:T(8,128)(2,1)} %bitcast.27, bf16[2,4096,128]{2,1,0:T(8,128)(2,1)} %bitcast.28, f32[2,6,64,8,128]{4,3,2,1,0:T(8,128)} %bitcast.26, f32[2,7,64,256]{3,2,1,0:T(8,128)} %cells.1, ...), custom_call_target="tpu_custom_call" | custom-call | tf_op jit(solution)/shard_map/pallas_call | solution.py:399
  75.9 2.3 %shard_map.95 = (bf16[2,4096,128]{2,1,0:T(8,128)(2,1)}, bf16[2,4096,128]{2,1,0:T(8,128)(2,1)}, f32[6,4,16,256]{3,2,1,0:T(8,128)}) custom-call(bf16[2,4096,128]{2,1,0:T(8,128)(2,1)S(1)} %get-tuple-element.9.rec, bf16[2,4096,128]{2,1,0:T(8,128)(2,1)S(1)} %get-tuple-element.10.inp, f32[6,4,16,256]{3,2,1,0:T(8,128)S(1)} %get-tuple-element.11.igrad), custom_call_target="tpu_custom_call" | custom-call | tf_op jit(solution)/shard_map/pallas_call | solution.py:441

commit v5 on v4

--- a/solution.py
+++ b/solution.py
@@ -289,7 +289,7 @@
         def _():
             store(2, t0, dgs[0, t0], 1)
 
-        @pl.when(d % 2 == 1)
+        @pl.when(jnp.logical_and(d > 1, d % 2 == 1))
         def _():
             weight_grads(1, t1)
 
@@ -307,9 +307,14 @@
         def _():
             scatter(2, t0)
 
-        @pl.when(d > 1)
-        def _():
-            pass_on(2, t0 + 1, t0 + 1)
+        @pl.when(d == 1)
+        def _():
+            weight_grads(1, t1)
+
+        @pl.when(d == T - 1)
+        def _():
+            for t in range(T - 1, 1, -1):
+                pass_on(2, t, t)
 
         return 0
 

time: 78.2 us -> 79.2 us (1.013)
  Pallas kernels: 77.5 us -> 78.3 us
    pallas_call x1, Pallas kernels: 75.2 us -> 76.1 us  [local(): pl.pallas_call(kernel, out_shape=(vmem((2, 8 * J, 128), BF16), vmem((2, 8...]
where the time goes in v5:
time: 79.2 us; the launch traced here: 79.1 us
  Pallas kernels  78.3 us (99%)
  between operations  0.8 us (1%)
    pallas_call x1, Pallas kernels, local(): pl.pallas_call(kernel, out_shape=(vmem((2, 8 * J, 128), BF16), vmem((2, 8...  76.1 us
    pallas_call x1, Pallas kernels, local(): pl.pallas_call(flush, out_shape=tuple((jax.ShapeDtypeStruct(x.shape, x.dt...  2.27 us

profile of v5, /device:TPU:1, one launch (start us, length us, event | category | flops | bytes accessed | tf_op | source)
XLA Modules:
  0.0 79.1 jit_solution(6266069233093843620)
XLA Ops:
  0.6 76.1 %shard_map.94 = (bf16[2,4096,128]{2,1,0:T(8,128)(2,1)S(1)}, bf16[2,4096,128]{2,1,0:T(8,128)(2,1)S(1)}, f32[6,4,16,256]{3,2,1,0:T(8,128)S(1)}) custom-call(bf16[2,4096,128]{2,1,0:T(8,128)(2,1)} %bitcast.27, bf16[2,4096,128]{2,1,0:T(8,128)(2,1)} %bitcast.28, f32[2,6,64,8,128]{4,3,2,1,0:T(8,128)} %bitcast.26, f32[2,7,64,256]{3,2,1,0:T(8,128)} %cells.1, ...), custom_call_target="tpu_custom_call" | custom-call | tf_op jit(solution)/shard_map/pallas_call | solution.py:404
  76.7 2.3 %shard_map.95 = (bf16[2,4096,128]{2,1,0:T(8,128)(2,1)}, bf16[2,4096,128]{2,1,0:T(8,128)(2,1)}, f32[6,4,16,256]{3,2,1,0:T(8,128)}) custom-call(bf16[2,4096,128]{2,1,0:T(8,128)(2,1)S(1)} %get-tuple-element.9.rec, bf16[2,4096,128]{2,1,0:T(8,128)(2,1)S(1)} %get-tuple-element.10.inp, f32[6,4,16,256]{3,2,1,0:T(8,128)S(1)} %get-tuple-element.11.igrad), custom_call_target="tpu_custom_call" | custom-call | tf_op jit(solution)/shard_map/pallas_call | solution.py:446
